TPU v7x, 32 devices: a whole 2x2x4 slice. The times are simulated.
32 devices in a mesh: seq: 8 (over y, x, core), fsdp: 4 (over z).
Axes of the slice: x: 2, y: 2, z: 4, core: 2. Of those that a mesh axis runs over, the one named last changes fastest.
Arguments:
- hidden: bfloat16 [4096, 8192], P(('seq', 'fsdp')), may hold values from -6 to 6
- kv_blocks: bfloat16 [8192, 1024], P('fsdp'), may hold values from -0.0625 to 0.0625
- kv_scale: float32 [64, 8], P('fsdp'), may hold values from 0.5 to 2
- queries: bfloat16 [4096, 4096], P(('seq', 'fsdp')), may hold values from -24 to 24
- grad_out: bfloat16 [4096, 4096], P(('seq', 'fsdp')), may hold values from -6 to 6
Outputs:
- attn_out: bfloat16 [4096, 4096], P(('seq', 'fsdp'))
- grad_queries: bfloat16 [4096, 4096], P(('seq', 'fsdp'))
- grad_hidden: bfloat16 [4096, 8192], P(('seq', 'fsdp'))
- weight_grad: float32 [8192, 1024], P('fsdp')
All inputs are finite; a program needn't handle non-finite values.
Results may differ from a plain program's by a relative error of at most 0.0075.
The roundings to bfloat16 on the way count: a program that leaves them out, or rounds other values in their place, can miss the bound.
Values may be sent and summed in bfloat16 or wider, within the bound.
A program may use at most 128 MiB of HBM per device.

v0:
```python
import functools

import jax
import jax.numpy as jnp
from jax import lax
from jax.experimental import pallas as pl
from jax.experimental.pallas import tpu as pltpu
from jax.sharding import PartitionSpec as P

HEADS = 32
KV_HEADS = 4
HEAD = 128
QB = 128


NEG = -1e30
PLANNED = (4, 4, 8)
(SEND, FORWARD, BEGIN, CUBE, PAIR, LAND, PROJECT, ATTEND, SETTLE, WIDEN, SHARE) = range(11)
(PRODUCT, HOP, REDUCE, EXPAND, RELAY, FINISH, SPREAD, HIDDEN, TURN) = range(11, 20)
VMEM_LIMIT = 50 << 20
WIDE = (2,)
ORDER = (
    (HIDDEN, 3), (SEND, 1), (FORWARD, 1, 0), (FORWARD, 0, 0), (BEGIN, 1, 0), (SEND, 2), (FORWARD, 0, 1), (TURN, 3),
    (BEGIN, 0, 0), (BEGIN, 0, 1), (SEND, 3), (CUBE, 1, 0), (CUBE, 0, 0), (FORWARD, 2, 0), (FORWARD, 0, 2),
    (BEGIN, 2, 0), (FORWARD, 1, 1), (BEGIN, 0, 2), (CUBE, 0, 1), (FORWARD, 1, 2), (PAIR, 0, 2), (CUBE, 2, 0),
    (BEGIN, 1, 2), (FORWARD, 2, 2), (BEGIN, 2, 2), (PAIR, 2, 0), (PAIR, 0, 0), (FORWARD, 1, 3), (BEGIN, 1, 3),
    (PAIR, 0, 1), (BEGIN, 1, 1), (FORWARD, 0, 3), (PAIR, 1, 0), (LAND, 0, 1), (LAND, 0, 0), (LAND, 2, 0),
    (FORWARD, 2, 1), (BEGIN, 0, 3), (BEGIN, 2, 1), (PAIR, 1, 2), (PAIR, 2, 2), (LAND, 1, 0), (FORWARD, 2, 3),
    (PROJECT, 0), (BEGIN, 2, 3), (LAND, 0, 2), (LAND, 2, 2), (LAND, 1, 2), (CUBE, 1, 3), (CUBE, 0, 3), (PROJECT, 2),
    (CUBE, 2, 3), (ATTEND, 0), (CUBE, 2, 1), (CUBE, 1, 1), (PAIR, 0, 3), (ATTEND, 2), (SETTLE, 0), (PAIR, 1, 3),
    (PAIR, 2, 3), (TURN, 0), (HIDDEN, 2), (LAND, 1, 3), (LAND, 0, 3), (WIDEN, 0), (PAIR, 1, 1), (HIDDEN, 1),
    (PAIR, 2, 1), (LAND, 2, 3), (PROJECT, 3), (LAND, 1, 1), (LAND, 2, 1), (PROJECT, 1), (ATTEND, 3), (TURN, 2),
    (SHARE, 0), (ATTEND, 1), (SETTLE, 2), (TURN, 1), (PRODUCT, 0), (WIDEN, 2), (SHARE, 2), (PRODUCT, 2), (SETTLE, 1),
    (SETTLE, 3), (HOP, 0, 1), (WIDEN, 1), (HOP, 0, 2), (SHARE, 1), (WIDEN, 3), (PRODUCT, 1), (HOP, 2, 1), (REDUCE, 0),
    (SPREAD, 3), (EXPAND, 0), (SHARE, 3), (HOP, 2, 2), (SPREAD, 0), (HOP, 1, 1), (REDUCE, 2), (HOP, 1, 2),
    (PRODUCT, 3), (EXPAND, 2), (RELAY, 0), (REDUCE, 1), (HOP, 3, 1), (RELAY, 2), (HOP, 3, 2), (EXPAND, 1),
    (REDUCE, 3), (EXPAND, 3), (RELAY, 1), (SPREAD, 2), (SPREAD, 1), (FINISH, 2), (FINISH, 0), (RELAY, 3), (FINISH, 1),
    (FINISH, 3),
)


def shifted(block, axis, distance):
    devices = range(lax.axis_size(axis))
    route = [(i - distance, i) for i in devices if i - distance in devices]
    return lax.ppermute(block, axis, route)


def attend_kernel(reach, q_ref, g_ref, k_ref, v_ref, out_ref, dq_ref, dk_ref, dv_ref):
    tok = q_ref.shape[0]
    group = q_ref.shape[1] // HEAD
    count = k_ref.shape[0]
    span = reach * tok
    factor = 1.0 / float(HEAD) ** 0.5
    base = (lax.axis_index("seq") * lax.axis_size("fsdp") + lax.axis_index("fsdp")) * tok
    row = lax.broadcasted_iota(jnp.int32, (tok, count), 0)
    col = lax.broadcasted_iota(jnp.int32, (tok, count), 1)
    allowed = (col > row) & (col <= row + span) & (col >= span - base)
    keys = k_ref[...]
    values = v_ref[...]
    nt = (((1,), (1,)), ((), ()))
    tn = (((0,), (0,)), ((), ()))
    ps, ds, qs, gs = [], [], [], []
    for h in range(group):
        cut = slice(h * HEAD, (h + 1) * HEAD)
        q = q_ref[:, cut]
        g = g_ref[:, cut]
        scores = lax.dot_general(q, keys, nt, preferred_element_type=jnp.float32) * factor
        scores = jnp.where(allowed, scores, NEG)
        expd = jnp.exp(scores - jnp.max(scores, axis=-1, keepdims=True))
        probs = expd * (1.0 / jnp.sum(expd, axis=-1, keepdims=True))
        probs_b = probs.astype(jnp.bfloat16)
        out_ref[:, cut] = jnp.dot(probs_b, values, preferred_element_type=jnp.float32).astype(jnp.bfloat16)
        dprobs = lax.dot_general(g, values, nt, preferred_element_type=jnp.float32)
        delta = jnp.sum(probs * dprobs, axis=-1, keepdims=True)
        dscores = (probs * (dprobs - delta) * factor).astype(jnp.bfloat16)
        dq_ref[:, cut] = jnp.dot(dscores, keys, preferred_element_type=jnp.float32).astype(jnp.bfloat16)
        ps.append(probs_b)
        ds.append(dscores)
        qs.append(q)
        gs.append(g)
    cat = lambda parts: jnp.concatenate(parts, axis=0)
    dk_ref[...] = lax.dot_general(cat(ds), cat(qs), tn, preferred_element_type=jnp.float32)
    dv_ref[...] = lax.dot_general(cat(ps), cat(gs), tn, preferred_element_type=jnp.float32)


def attend(queries, window, grad_out, reach):
    tok, width = queries.shape
    count = window.shape[0]
    heads = window.shape[1] // (2 * HEAD)
    wide = pl.BlockSpec((tok, width // heads), lambda i: (0, i))
    key = pl.BlockSpec((count, HEAD), lambda i: (0, i))
    value = pl.BlockSpec((count, HEAD), lambda i: (0, i + heads))
    out, dq, dk, dv = pl.pallas_call(
        functools.partial(attend_kernel, reach),
        grid=(heads,),
        in_specs=[wide, wide, key, value],
        out_specs=[wide, wide, key, key],
        out_shape=[
            jax.ShapeDtypeStruct((tok, width), jnp.bfloat16),
            jax.ShapeDtypeStruct((tok, width), jnp.bfloat16),
            jax.ShapeDtypeStruct((count, heads * HEAD), jnp.float32),
            jax.ShapeDtypeStruct((count, heads * HEAD), jnp.float32),
        ],
        cost_estimate=pl.CostEstimate(flops=12 * tok * width * count, bytes_accessed=8 * tok * width, transcendentals=0),
        name="attend",
    )(queries, grad_out, window, window)
    return out, dq, jnp.concatenate([dk, dv], axis=1)


def flipped(index, mask):
    for place in range(mask.bit_length()):
        if mask >> place & 1:
            index = index + (1 << place) * (1 - 2 * (index // (1 << place) % 2))
    return index


def orders_of(bits):
    return (list(range(1, bits)) + [0], list(range(bits - 1, 0, -1)) + [0])


def project_kernel(seqs, groups, hid_ref, blk_ref, sc_ref, out_ref, kv_ref, col_ref, w_ref, acc, zsend, zrecv, qsend, qrecv, csend, crecv, wsem):
    s = lax.axis_index("seq")
    z = lax.axis_index("fsdp")
    rows = blk_ref.shape[0]
    unit = rows // seqs
    half = unit // 2
    bits = seqs.bit_length() - 1
    chunk = min(512, rows)

    def scale_block(i, carry):
        at = pl.multiple_of(i * QB, QB)
        block = blk_ref[pl.ds(at, QB), :].astype(jnp.float32) * sc_ref[pl.ds(i, 1), :]
        w_ref[pl.ds(pl.multiple_of(z * rows + at, QB), QB), :] = block.astype(jnp.bfloat16)
        return carry

    lax.fori_loop(0, rows // QB, scale_block, 0)

    def line_copy(shard, up):
        piece = w_ref.at[pl.ds(pl.multiple_of(shard * rows + s * unit, 16), unit), :]
        return pltpu.make_async_remote_copy(
            src_ref=piece,
            dst_ref=piece,
            send_sem=zsend.at[up, shard],
            recv_sem=zrecv.at[shard],
            device_id=(s, z + 1 if up else z - 1),
            device_id_type=pl.DeviceIdType.MESH,
        )

    def cube_copy(turn, shard, order, step, which, incoming):
        bit = order[step]
        mask = 0
        for k in range(step):
            if which >> k & 1:
                mask |= 1 << order[k]
        h = 0 if order is orders[0] else 1
        owner = flipped(s, mask | (1 << bit) if incoming else mask)
        piece = w_ref.at[pl.ds(pl.multiple_of(shard * rows + owner * unit + h * half, 16), half), :]
        slot = (1 << step) - 1 + which
        return pltpu.make_async_remote_copy(
            src_ref=piece,
            dst_ref=piece,
            send_sem=qsend.at[turn, h, slot],
            recv_sem=qrecv.at[turn, h, slot],
            device_id=(flipped(s, 1 << bit), z),
            device_id_type=pl.DeviceIdType.MESH,
        )

    orders = orders_of(bits)
    near = jnp.minimum(z, groups - 1 - z)

    def shard_at(turn):
        step = turn // 2 + 1
        paired = z - step if turn % 2 == 0 else z + step
        far = turn - near + 1
        single = jnp.where(z > groups - 1 - z, z - far, z + far)
        return jnp.where(turn < 2 * near, paired, single)

    shards = [shard_at(turn) for turn in range(groups - 1)]

    @pl.when(z < groups - 1)
    def _():
        line_copy(z, 1).start()

    @pl.when(z > 0)
    def _():
        line_copy(z, 0).start()

    def column_copy(gap, incoming):
        other = (z - gap + groups) % groups if incoming else (z + gap) % groups
        part = pl.multiple_of(other * rows, 128)
        return pltpu.make_async_remote_copy(
            src_ref=hid_ref.at[:, pl.ds(part, rows)],
            dst_ref=col_ref.at[other if incoming else z],
            send_sem=csend.at[gap - 1],
            recv_sem=crecv.at[gap - 1],
            device_id=(s, other),
            device_id_type=pl.DeviceIdType.MESH,
        )

    acc[...] = jnp.zeros_like(acc)

    def store_copy(turn, shard):
        part = pl.ds(pl.multiple_of(shard * rows, 16), rows)
        return pltpu.make_async_copy(w_ref.at[part, :], out_ref.at[part, :], wsem.at[turn])

    def multiply(shard):
        def part(i, carry):
            at = pl.multiple_of(shard * rows + i * chunk, 128)
            acc[...] += jnp.dot(
                hid_ref[:, pl.ds(at, chunk)], w_ref[pl.ds(at, chunk), :], preferred_element_type=jnp.float32
            )
            return carry

        lax.fori_loop(0, rows // chunk, part, 0)

    multiply(z)
    store_copy(groups - 1, z).start()
    col_ref[z] = hid_ref[:, pl.ds(pl.multiple_of(z * rows, 128), rows)]
    for tick in range(groups - 1 + bits):
        for stage in range(bits, -1, -1):
            turn = tick - stage
            if turn < 0 or turn >= groups - 1:
                continue
            shard = shards[turn]
            if stage == 0:
                line_copy(shard, 0).wait_recv()

                @pl.when((shard < z) & (z < groups - 1))
                def _():
                    line_copy(shard, 1).start()

                @pl.when((shard > z) & (z > 0))
                def _():
                    line_copy(shard, 0).start()
            else:
                for order in orders:
                    for which in range(1 << (stage - 1)):
                        cube_copy(turn, shard, order, stage - 1, which, True).wait_recv()
            if stage < bits:
                for order in orders:
                    for which in range(1 << stage):
                        cube_copy(turn, shard, order, stage, which, False).start()
            else:
                multiply(shard)
                store_copy(turn, shard).start()
        if tick == groups - 2:
            for gap in range(1, groups):
                column_copy(gap, False).start()
    kv_ref[...] = acc[...].astype(jnp.bfloat16)
    for turn in range(groups - 1):
        store_copy(turn, shards[turn]).wait()
    store_copy(groups - 1, z).wait()
    for gap in range(1, groups):
        column_copy(gap, True).wait_recv()
        column_copy(gap, False).wait_send()
    for shard in range(groups):

        @pl.when((shard <= z) & (z < groups - 1))
        def _():
            line_copy(shard, 1).wait_send()

        @pl.when((shard >= z) & (z > 0))
        def _():
            line_copy(shard, 0).wait_send()

    for turn in range(groups - 1):
        for order in orders:
            for stage in range(bits):
                for which in range(1 << stage):
                    cube_copy(turn, shards[turn], order, stage, which, False).wait_send()


def project(hidden, kv_blocks, kv_scale):
    seqs = lax.axis_size("seq")
    groups = lax.axis_size("fsdp")
    tok, width = hidden.shape
    cols = kv_blocks.shape[1]
    spread = jnp.repeat(kv_scale, QB, axis=1)
    vmem = pl.BlockSpec(memory_space=pltpu.VMEM)
    return pl.pallas_call(
        functools.partial(project_kernel, seqs, groups),
        out_shape=[
            jax.ShapeDtypeStruct((width, cols), jnp.bfloat16),
            jax.ShapeDtypeStruct((tok, cols), jnp.bfloat16),
            jax.ShapeDtypeStruct((groups, tok, kv_blocks.shape[0]), jnp.bfloat16),
        ],
        in_specs=[vmem] * 3,
        out_specs=[pl.BlockSpec(memory_space=pl.ANY), vmem, vmem],
        scratch_shapes=[
            pltpu.VMEM((width, cols), jnp.bfloat16),
            pltpu.VMEM((tok, cols), jnp.float32),
            pltpu.SemaphoreType.DMA((2, groups)),
            pltpu.SemaphoreType.DMA((groups,)),
            pltpu.SemaphoreType.DMA((groups - 1, 2, seqs - 1)),
            pltpu.SemaphoreType.DMA((groups - 1, 2, seqs - 1)),
            pltpu.SemaphoreType.DMA((groups - 1,)),
            pltpu.SemaphoreType.DMA((groups - 1,)),
            pltpu.SemaphoreType.DMA((groups,)),
        ],
        compiler_params=pltpu.CompilerParams(has_side_effects=True),
        name="project",
    )(hidden, kv_blocks, spread)


def finish_kernel(
    seqs, groups, reach, back_ref, own_ref, in_ref, col_ref, gh_ref, wg_ref,
    w_ref, wsem, ret, every, inside, acc, sends, recvs, hsend, hrecv, gsend, grecv, rsend, rrecv, asend, arecv,
):
    s = lax.axis_index("seq")
    z = lax.axis_index("fsdp")
    linear = s * groups + z
    devices = seqs * groups
    tok, cols = own_ref.shape
    rows = col_ref.shape[1]
    bits = seqs.bit_length() - 1
    mesh_id = pl.DeviceIdType.MESH
    load = pltpu.make_async_copy(in_ref, w_ref, wsem)
    load.start()

    def halo_copy(offset, incoming):
        other = linear + offset if incoming else linear - offset
        return pltpu.make_async_remote_copy(
            src_ref=back_ref.at[pl.ds((reach - offset) * tok, tok), :],
            dst_ref=ret.at[offset - 1],
            send_sem=hsend.at[offset - 1],
            recv_sem=hrecv.at[offset - 1],
            device_id=(other // groups, other % groups),
            device_id_type=mesh_id,
        )

    for offset in range(1, reach + 1):

        @pl.when(linear >= offset)
        def _():
            halo_copy(offset, False).start()

    for offset in range(1, reach + 1):

        @pl.when(linear + offset < devices)
        def _():
            halo_copy(offset, True).wait_recv()

        @pl.when(linear + offset >= devices)
        def _():
            ret[offset - 1] = jnp.zeros((tok, cols), jnp.bfloat16)

    total = own_ref[...]
    seg = total
    for offset in range(1, reach + 1):
        piece = ret[offset - 1].astype(jnp.float32)
        total = total + piece
        seg = seg + piece * jnp.where(z + offset < groups, 1.0, 0.0)
    every[z] = total.astype(jnp.bfloat16)
    inside[...] = seg.astype(jnp.bfloat16)

    def gather_copy(gap, incoming):
        other = (z - gap + groups) % groups if incoming else (z + gap) % groups
        block = every.at[other if incoming else z]
        return pltpu.make_async_remote_copy(
            src_ref=block,
            dst_ref=block,
            send_sem=gsend.at[gap - 1],
            recv_sem=grecv.at[gap - 1],
            device_id=(s, other),
            device_id_type=mesh_id,
        )

    for gap in range(1, groups):
        gather_copy(gap, False).start()

    load.wait()
    wide = 512

    def spread(i, carry):
        at = pl.multiple_of(i * wide, wide)
        gh_ref[:, pl.ds(at, wide)] = lax.dot_general(
            inside[...], w_ref[pl.ds(at, wide), :], (((1,), (1,)), ((), ())), preferred_element_type=jnp.float32
        ).astype(jnp.bfloat16)
        return carry

    lax.fori_loop(0, w_ref.shape[0] // wide, spread, 0)
    for gap in range(1, groups):
        gather_copy(gap, True).wait_recv()

    big = rows // 2
    tile = min(256, big)
    low = s % 2
    sibling = flipped(s, 1)
    grads = every[...].reshape(groups * tok, cols)

    def product(at):
        return lax.dot_general(
            col_ref[:, pl.ds(at, tile)], grads, (((0,), (0,)), ((), ())), preferred_element_type=jnp.float32
        )

    def theirs(i, carry):
        at = pl.multiple_of(i * tile, tile)
        sends[0][pl.ds(at, tile), :] = product(pl.multiple_of((1 - low) * big + at, tile)).astype(jnp.bfloat16)
        return carry

    lax.fori_loop(0, big // tile, theirs, 0)

    def reduce_copy(step, h, peer):
        cut = slice(None) if h is None else pl.ds(h * (cols // 2), cols // 2)
        return pltpu.make_async_remote_copy(
            src_ref=sends[step].at[:, cut] if h is not None else sends[step],
            dst_ref=recvs[step].at[:, cut] if h is not None else recvs[step],
            send_sem=rsend.at[step, h or 0],
            recv_sem=rrecv.at[step, h or 0],
            device_id=(peer, z),
            device_id_type=mesh_id,
        )

    reduce_copy(0, None, sibling).start()

    def mine(i, carry):
        at = pl.multiple_of(i * tile, tile)
        acc[pl.ds(at, tile), :] = product(pl.multiple_of(low * big + at, tile))
        return carry

    lax.fori_loop(0, big // tile, mine, 0)
    reduce_copy(0, None, sibling).wait_recv()

    def fold(i, carry):
        at = pl.multiple_of(i * tile, tile)
        acc[pl.ds(at, tile), :] += recvs[0][pl.ds(at, tile), :].astype(jnp.float32)
        return carry

    lax.fori_loop(0, big // tile, fold, 0)
    orders = (list(range(1, bits)), list(range(bits - 1, 0, -1)))
    offsets = [[0], [0]]
    side = cols // 2
    for step in range(1, bits):
        size = rows >> (step + 1)
        for h in range(2):
            place = orders[h][step - 1]
            bit = s // (1 << place) % 2
            start = offsets[h][-1]
            away = pl.multiple_of(start + (1 - bit) * size, 16)
            sends[step][:, h * side : (h + 1) * side] = acc[
                pl.ds(away, size), h * side : (h + 1) * side
            ].astype(jnp.bfloat16)
            reduce_copy(step, h, flipped(s, 1 << place)).start()
            offsets[h].append(start + bit * size)
        for h in range(2):
            place = orders[h][step - 1]
            reduce_copy(step, h, flipped(s, 1 << place)).wait_recv()
            keep = pl.ds(pl.multiple_of(offsets[h][-1], 16), size)
            cut = slice(h * side, (h + 1) * side)
            acc[keep, cut] += recvs[step][:, cut].astype(jnp.float32)
    size = rows >> bits
    for h in range(2):
        at = offsets[h][-1]
        cut = slice(h * side, (h + 1) * side)
        wg_ref[pl.ds(pl.multiple_of(low * big + at, 16), size), cut] = acc[
            pl.ds(pl.multiple_of(at, 16), size), cut
        ].astype(jnp.bfloat16)

    def spread_copy(step, h, incoming):
        place = orders[h][step - 1]
        bit = s // (1 << place) % 2
        size = rows >> (step + 1)
        at = low * big + offsets[h][step - 1] + ((1 - bit) if incoming else bit) * size
        block = wg_ref.at[pl.ds(pl.multiple_of(at, 16), size), pl.ds(h * side, side)]
        return pltpu.make_async_remote_copy(
            src_ref=block,
            dst_ref=block,
            send_sem=asend.at[step, h],
            recv_sem=arecv.at[step, h],
            device_id=(flipped(s, 1 << place), z),
            device_id_type=mesh_id,
        )

    for step in range(bits - 1, 0, -1):
        for h in range(2):
            spread_copy(step, h, False).start()
        for h in range(2):
            spread_copy(step, h, True).wait_recv()

    def last_copy(incoming):
        block = wg_ref.at[pl.ds(pl.multiple_of(((1 - low) if incoming else low) * big, 16), big), :]
        return pltpu.make_async_remote_copy(
            src_ref=block,
            dst_ref=block,
            send_sem=asend.at[0, 0],
            recv_sem=arecv.at[0, 0],
            device_id=(sibling, z),
            device_id_type=mesh_id,
        )

    last_copy(False).start()
    last_copy(True).wait_recv()
    for offset in range(1, reach + 1):

        @pl.when(linear >= offset)
        def _():
            halo_copy(offset, False).wait_send()

    for gap in range(1, groups):
        gather_copy(gap, False).wait_send()
    reduce_copy(0, None, sibling).wait_send()
    for step in range(1, bits):
        for h in range(2):
            reduce_copy(step, h, flipped(s, 1 << orders[h][step - 1])).wait_send()
            spread_copy(step, h, False).wait_send()
    last_copy(False).wait_send()


def finish(back, own, weights, columns, reach):
    seqs = lax.axis_size("seq")
    groups = lax.axis_size("fsdp")
    tok, cols = own.shape
    rows = columns.shape[1]
    bits = seqs.bit_length() - 1
    vmem = pl.BlockSpec(memory_space=pltpu.VMEM)
    steps = [pltpu.VMEM((rows >> (k + 1), cols), jnp.bfloat16) for k in range(bits)]
    dma = pltpu.SemaphoreType.DMA
    return pl.pallas_call(
        functools.partial(finish_kernel, seqs, groups, reach),
        out_shape=[
            jax.ShapeDtypeStruct((tok, weights.shape[0]), jnp.bfloat16),
            jax.ShapeDtypeStruct((rows, cols), jnp.bfloat16),
        ],
        in_specs=[vmem, vmem, pl.BlockSpec(memory_space=pl.ANY), vmem],
        out_specs=[vmem] * 2,
        scratch_shapes=[
            pltpu.VMEM(weights.shape, jnp.bfloat16),
            dma(()),
            pltpu.VMEM((reach, tok, cols), jnp.bfloat16),
            pltpu.VMEM((groups, tok, cols), jnp.bfloat16),
            pltpu.VMEM((tok, cols), jnp.bfloat16),
            pltpu.VMEM((rows // 2, cols), jnp.float32),
            steps,
            steps,
            dma((reach,)),
            dma((reach,)),
            dma((groups - 1,)),
            dma((groups - 1,)),
            dma((bits, 2)),
            dma((bits, 2)),
            dma((bits, 2)),
            dma((bits, 2)),
        ],
        compiler_params=pltpu.CompilerParams(has_side_effects=True),
        name="finish",
    )(back, own, weights, columns)


def fused_kernel(
    seqs, groups, reach,
    hid_in, blk_in, sc_ref, q_in, g_in, ao, dq, gh, wgb,
    hid, blk, q_ref, g_ref, w_ref, win, back, ret, own, every, inside, hb, ht, part,
    ups, upr, dns, dnr, bias, lead_ref,
    lsem, zsend, zrecv, qsend, qrecv, csend, crecv, hsend, hrecv, ksend, krecv, bsend, brecv,
    esend, erecv, fsend, frecv, usend, urecv, dsend, drecv, wsend, wrecv, xsend, xrecv,
):
    s = lax.axis_index("seq")
    z = lax.axis_index("fsdp")
    linear = s * groups + z
    devices = seqs * groups
    tok, width = hid.shape
    rows, cols = blk.shape
    unit = rows // seqs
    bits = seqs.bit_length() - 1
    heads = cols // (2 * HEAD)
    duo = 2 * HEAD
    group = q_ref.shape[1] // HEAD // heads
    span = reach * tok
    last = groups - 1
    sibling = flipped(s, 1)
    peers = [m << 1 for m in range(1, seqs // 2)]
    nt = (((1,), (1,)), ((), ()))
    tn = (((0,), (0,)), ((), ()))
    mesh_id = pl.DeviceIdType.MESH

    def chunk(g):
        return pl.ds(g * duo, duo)

    def remote(src, dst, send, recv, to_s, to_z):
        return pltpu.make_async_remote_copy(
            src_ref=src, dst_ref=dst, send_sem=send, recv_sem=recv, device_id=(to_s, to_z), device_id_type=mesh_id
        )

    barrier = pltpu.get_barrier_semaphore()
    partners = [(None, flipped(s, m), z) for m in range(1, seqs)]
    partners += [(z < last, s, z + 1), (z > 0, s, z - 1)]
    for offset in range(1, reach + 1):
        up, down = linear + offset, linear - offset
        partners.append((up < devices, up // groups, up % groups))
        partners.append((down >= 0, down // groups, down % groups))

    def greet(to_s, to_z):
        pl.semaphore_signal(barrier, inc=1, device_id=(to_s, to_z), device_id_type=mesh_id)

    for present, to_s, to_z in partners:
        if present is None:
            greet(to_s, to_z)
        else:
            pl.when(present)(functools.partial(greet, to_s, to_z))

    mine = pl.ds(pl.multiple_of(s * unit, 16), unit)
    first = pltpu.make_async_copy(blk_in.at[mine, :], lead_ref, lsem.at[0])
    first.start()
    loads = [
        pltpu.make_async_copy(blk_in, blk, lsem.at[1]),
        pltpu.make_async_copy(hid_in, hid, lsem.at[2]),
        pltpu.make_async_copy(q_in, q_ref, lsem.at[3]),
        pltpu.make_async_copy(g_in, g_ref, lsem.at[4]),
    ]
    loads[1].start()

    def scale_block(i, source, at):
        to = pl.ds(pl.multiple_of(z * rows + i * QB, QB), QB)
        for j in range(cols // QB):
            block = source[pl.ds(at, QB), j * QB : (j + 1) * QB].astype(jnp.float32) * sc_ref[j, i]
            side = j // heads * HEAD
            w_ref[j % heads, to, side : side + HEAD] = block.astype(jnp.bfloat16)

    near = jnp.minimum(z, last - z)

    def shard_at(turn):
        step = turn // 2 + 1
        paired = z - step if turn % 2 == 0 else z + step
        far = turn - near + 1
        single = jnp.where(z > last - z, z - far, z + far)
        return jnp.where(turn < 2 * near, paired, single)

    shards = [shard_at(turn) for turn in range(groups - 1)]
    orders = (list(range(1, bits)), list(range(bits - 1, 0, -1)))

    def span_of(g, shard, owner, h=None):
        at = shard * rows + owner * unit + (0 if h is None else h * (unit // 2))
        return w_ref.at[g, pl.ds(pl.multiple_of(at, 16), unit if h is None else unit // 2), :]

    def kinds(g):
        return range(3 if g in WIDE else 1)

    def line_copy(shard, up, g, kind):
        if kind == 0:
            piece = span_of(g, shard, s)
        else:
            piece = span_of(g, shard, flipped(s, 1 << orders[kind - 1][0]), kind - 1)
        return remote(piece, piece, zsend.at[up, shard], zrecv.at[shard, g], s, z + 1 if up else z - 1)

    def cube_copy(turn, g, h, step, which, incoming):
        order = orders[h]
        bit = order[step]
        mask = 0
        for k in range(step):
            if which >> k & 1:
                mask |= 1 << order[k]
        piece = span_of(g, shards[turn], flipped(s, mask | (1 << bit) if incoming else mask), h)
        return remote(piece, piece, qsend.at[0], qrecv.at[turn, g, step], flipped(s, 1 << bit), z)

    def pair_copy(turn, g, m, incoming):
        piece = span_of(g, shards[turn], flipped(s, (m << 1) | 1 if incoming else m << 1))
        return remote(piece, piece, csend.at[0], crecv.at[turn, g], sibling, z)

    def hidden_copy(d, m):
        peer = flipped(s, m)
        return remote(
            hid.at[:, pl.ds(pl.multiple_of(d * rows + peer * unit, 128), unit)], hb.at[s, d],
            hsend.at[0], hrecv.at[d], peer, z,
        )

    def hidden_send(d):
        for m in range(1, seqs):
            hidden_copy(d, m).start()

    def hidden_wait(d):
        whole = hb.at[pl.ds(0, seqs - 1), d]
        remote(whole, whole, hsend.at[0], hrecv.at[d], s, z).wait_recv()

    def own_send(g):
        for kind in kinds(g):

            @pl.when(z < last)
            def _():
                line_copy(z, 1, g, kind).start()

            @pl.when(z > 0)
            def _():
                line_copy(z, 0, g, kind).start()

    def forward(turn, g):
        shard = shards[turn]
        whole = w_ref.at[g, pl.ds(0, unit * (2 if g in WIDE else 1)), :]
        remote(whole, whole, zsend.at[0, shard], zrecv.at[shard, g], s, z).wait_recv()
        for kind in kinds(g):

            @pl.when((shard < z) & (z < last))
            def _():
                line_copy(shard, 1, g, kind).start()

            @pl.when((shard > z) & (z > 0))
            def _():
                line_copy(shard, 0, g, kind).start()

    def cube_wait(turn, g, step):
        whole = w_ref.at[g, pl.ds(0, unit << step), :]
        remote(whole, whole, qsend.at[0], qrecv.at[turn, g, step], s, z).wait_recv()

    def cube_send(turn, g, step):
        for which in range(1 << step):
            for h in range(2):
                cube_copy(turn, g, h, step, which, False).start()

    def pair_send(turn, g):
        for m in range(seqs // 2):
            pair_copy(turn, g, m, False).start()

    def pair_wait(turn, g):
        whole = w_ref.at[g, pl.ds(0, unit * (seqs // 2)), :]
        remote(whole, whole, csend.at[0], crecv.at[turn, g], s, z).wait_recv()

    def begin(turn, g):
        if g not in WIDE:
            cube_send(turn, g, 0)
        else:
            cube_send(turn, g, 1)

    def cube_next(turn, g):
        cube_wait(turn, g, 0)
        cube_send(turn, g, 1)

    def pair_send_after(turn, g):
        cube_wait(turn, g, bits - 2)
        pair_send(turn, g)

    first.wait()
    loads[0].start()
    lead = unit // QB
    for i in range(lead):
        scale_block(s * lead + i, lead_ref, i * QB)
    pl.semaphore_wait(barrier, sum(1 if present is None else jnp.where(present, 1, 0) for present, _, _ in partners))

    own_send(0)
    loads[1].wait()
    hidden_send(0)
    loads[0].wait()

    def scale_rest(i, carry):
        place = (s * lead + lead + i) % (rows // QB)
        scale_block(place, blk, pl.multiple_of(place * QB, QB))
        return carry

    lax.fori_loop(0, rows // QB - lead, scale_rest, 0)
    loads[2].start()
    loads[3].start()
    row = lax.broadcasted_iota(jnp.int32, (tok, tok), 0)
    col = lax.broadcasted_iota(jnp.int32, (tok, tok), 1)
    bias[...] = jnp.where((col > row) & (linear < reach), NEG, 0.0)
    for offset in range(1, reach + 1):

        @pl.when(linear < offset)
        def _():
            win[(reach - offset) * tok : (reach - offset + 1) * tok, :] = jnp.zeros((tok, cols), jnp.bfloat16)

        @pl.when(linear + offset >= devices)
        def _():
            ret[offset - 1] = jnp.zeros((tok, cols), jnp.bfloat16)

    @pl.when(z == 0)
    def _():
        for g in range(heads):
            upr[g, 0] = jnp.zeros((unit, duo), jnp.bfloat16)

    @pl.when(z == last)
    def _():
        for g in range(heads):
            dnr[g, last] = jnp.zeros((unit, duo), jnp.bfloat16)

    deep = min(1024, width)

    def project_chunk(g):
        def step(i, total):
            at = pl.multiple_of(i * deep, deep)
            return total + jnp.dot(hid[:, pl.ds(at, deep)], w_ref[g, pl.ds(at, deep), :], preferred_element_type=jnp.float32)

        total = lax.fori_loop(0, width // deep, step, jnp.zeros((tok, duo), jnp.float32))
        win[span:, g * duo : (g + 1) * duo] = total.astype(jnp.bfloat16)
        for offset in range(1, reach + 1):

            @pl.when(linear + offset < devices)
            def _():
                halo_copy(g, offset, False).start()

    def halo_copy(g, offset, incoming):
        other = linear - offset if incoming else linear + offset
        return remote(
            win.at[pl.ds(span, tok), chunk(g)], win.at[pl.ds((reach - offset) * tok, tok), chunk(g)],
            ksend.at[offset - 1], krecv.at[g, offset - 1], other // groups, other % groups,
        )

    def back_copy(g, offset, incoming):
        other = linear + offset if incoming else linear - offset
        return remote(
            back.at[offset - 1, :, chunk(g)], ret.at[offset - 1, :, chunk(g)],
            bsend.at[offset - 1], brecv.at[g, offset - 1], other // groups, other % groups,
        )

    factor = 1.0 / float(HEAD) ** 0.5
    cat = lambda parts: jnp.concatenate(parts, axis=0)

    def attend_chunk(g):
        for offset in range(1, reach + 1):

            @pl.when(linear >= offset)
            def _():
                halo_copy(g, offset, True).wait_recv()

        keys = win[:, g * duo : g * duo + HEAD]
        values = win[:, g * duo + HEAD : (g + 1) * duo]
        cuts = [slice(h * HEAD, (h + 1) * HEAD) for h in range(g * group, (g + 1) * group)]
        q = cat([q_ref[:, cut] for cut in cuts])
        go = cat([g_ref[:, cut] for cut in cuts])
        upper = cat([col > row] * group)
        scores = lax.dot_general(q, keys, nt, preferred_element_type=jnp.float32)
        dprobs = lax.dot_general(go, values, nt, preferred_element_type=jnp.float32)

        def folded(x):
            return [jnp.where(upper, x[:, :tok], x[:, span:])] + [x[:, j * tok : (j + 1) * tok] for j in range(1, reach)]

        def unfolded(x):
            zero = jnp.zeros_like(x[0])
            parts = [jnp.where(upper, x[0], zero)] + x[1:] + [jnp.where(upper, zero, x[0])]
            return jnp.concatenate([part.astype(jnp.bfloat16) for part in parts], axis=1)

        masks = [cat([bias[...]] * group)] + [jnp.where(linear < reach - j, NEG, 0.0) for j in range(1, reach)]
        scores = [x * factor + mask for x, mask in zip(folded(scores), masks)]
        dprobs = folded(dprobs)
        top = jnp.max(functools.reduce(jnp.maximum, scores), axis=-1, keepdims=True)
        expd = [jnp.exp(x - top) for x in scores]
        scale = 1.0 / jnp.sum(functools.reduce(jnp.add, expd), axis=-1, keepdims=True)
        probs = [x * scale for x in expd]
        delta = jnp.sum(functools.reduce(jnp.add, [p * d for p, d in zip(probs, dprobs)]), axis=-1, keepdims=True)
        probs_b = unfolded(probs)
        dscores = unfolded([p * (d - delta) * factor for p, d in zip(probs, dprobs)])
        out = jnp.dot(probs_b, values, preferred_element_type=jnp.float32).astype(jnp.bfloat16)
        gq = jnp.dot(dscores, keys, preferred_element_type=jnp.float32).astype(jnp.bfloat16)
        for i, cut in enumerate(cuts):
            ao[:, cut] = out[i * tok : (i + 1) * tok]
            dq[:, cut] = gq[i * tok : (i + 1) * tok]
        dk = lax.dot_general(dscores, q, tn, preferred_element_type=jnp.float32)
        dv = lax.dot_general(probs_b, go, tn, preferred_element_type=jnp.float32)
        for side, value in ((0, dk), (HEAD, dv)):
            cut = slice(g * duo + side, g * duo + side + HEAD)
            for offset in range(1, reach + 1):
                back[offset - 1, :, cut] = value[(reach - offset) * tok : (reach - offset + 1) * tok].astype(jnp.bfloat16)
            own[:, cut] = value[span:]
        for offset in range(1, reach + 1):

            @pl.when(linear >= offset)
            def _():
                back_copy(g, offset, False).start()

    def cube_mask(h, step, which):
        return sum(1 << orders[h][k] for k in range(step) if which >> k & 1)

    def every_copy(g, h, step, which):
        block = every.at[flipped(s, cube_mask(h, step, which)), pl.ds(h * (tok // 2), tok // 2), chunk(g)]
        return remote(block, block, esend.at[0], erecv.at[g, step], flipped(s, 1 << orders[h][step]), z)

    def every_send(g, step):
        for which in range(1 << step):
            for h in range(2):
                every_copy(g, h, step, which).start()

    def every_pair(g, m, incoming):
        block = every.at[flipped(s, m | 1 if incoming else m), :, chunk(g)]
        return remote(block, block, fsend.at[0], frecv.at[g], sibling, z)

    def settle(g):
        for offset in range(1, reach + 1):

            @pl.when(linear + offset < devices)
            def _():
                back_copy(g, offset, True).wait_recv()

        cut = slice(g * duo, (g + 1) * duo)
        total = own[:, cut]
        seg = total
        for offset in range(1, reach + 1):
            piece = ret[offset - 1, :, cut].astype(jnp.float32)
            total = total + piece
            seg = seg + piece * jnp.where(z + offset < groups, 1.0, 0.0)
        every[s, :, cut] = total.astype(jnp.bfloat16)
        inside[:, cut] = seg.astype(jnp.bfloat16)
        every_send(g, 0)
        every_pair(g, 0, False).start()

    def widen(g):
        whole = every.at[0, :, chunk(g)]
        remote(whole, whole, esend.at[0], erecv.at[g, 0], s, z).wait_recv()
        every_send(g, 1)

    def share(g):
        whole = every.at[pl.ds(0, 2), :, chunk(g)]
        remote(whole, whole, esend.at[0], erecv.at[g, 1], s, z).wait_recv()
        for m in peers:
            every_pair(g, m, False).start()

    def up_copy(g, d):
        return remote(ups.at[g, d], upr.at[g, d], usend.at[d], urecv.at[g, d], s, z + 1)

    def down_copy(g, d):
        return remote(dns.at[g, d], dnr.at[g, d], dsend.at[d], drecv.at[g, d], s, z - 1)

    def hop(g, k):
        @pl.when(z == k)
        def _():
            for d in range(last, k, -1):
                value = part[g, d]
                if k > 0:
                    up_copy(g, d).wait_recv()
                    value = value + upr[g, d].astype(jnp.float32)
                ups[g, d] = value.astype(jnp.bfloat16)
                up_copy(g, d).start()

        @pl.when(z == last - k)
        def _():
            for d in range(last - k):
                value = part[g, d]
                if k > 0:
                    down_copy(g, d).wait_recv()
                    value = value + dnr[g, d].astype(jnp.float32)
                dns[g, d] = value.astype(jnp.bfloat16)
                down_copy(g, d).start()

    def product(g):
        whole = every.at[pl.ds(0, seqs // 2), :, chunk(g)]
        remote(whole, whole, fsend.at[0], frecv.at[g], s, z).wait_recv()
        grads = every[:, :, g * duo : (g + 1) * duo].reshape(seqs * tok, duo)

        def step(d, carry):
            part[g, d] = jnp.dot(
                ht[pl.ds(pl.multiple_of(d * unit, 128), unit), :], grads, preferred_element_type=jnp.float32
            )
            return carry

        lax.fori_loop(0, groups, step, 0)
        hop(g, 0)

    def grad_copy(g, h, step, which):
        at = flipped(s, cube_mask(h, step, which)) * unit + h * (unit // 2)
        block = wgb.at[g, pl.ds(pl.multiple_of(at, 16), unit // 2), :]
        return remote(block, block, wsend.at[0], wrecv.at[g, step], flipped(s, 1 << orders[h][step]), z)

    def grad_send(g, step):
        for which in range(1 << step):
            for h in range(2):
                grad_copy(g, h, step, which).start()

    def grad_pair(g, m, incoming):
        owner = flipped(s, m | 1 if incoming else m)
        block = wgb.at[g, pl.ds(pl.multiple_of(owner * unit, 128), unit), :]
        return remote(block, block, xsend.at[0], xrecv.at[g], sibling, z)

    def reduce(g):
        @pl.when(z > 0)
        def _():
            up_copy(g, z).wait_recv()

        @pl.when(z < last)
        def _():
            down_copy(g, z).wait_recv()

        total = part[g, z] + upr[g, z].astype(jnp.float32) + dnr[g, z].astype(jnp.float32)
        wgb[g, pl.ds(pl.multiple_of(s * unit, 128), unit), :] = total.astype(jnp.bfloat16)
        grad_send(g, 0)
        grad_pair(g, 0, False).start()

    def expand(g):
        whole = wgb.at[g, pl.ds(0, unit), :]
        remote(whole, whole, wsend.at[0], wrecv.at[g, 0], s, z).wait_recv()
        grad_send(g, 1)

    def relay(g):
        whole = wgb.at[g, pl.ds(0, 2 * unit), :]
        remote(whole, whole, wsend.at[0], wrecv.at[g, 1], s, z).wait_recv()
        for m in peers:
            grad_pair(g, m, False).start()

    def finish_chunk(g):
        whole = wgb.at[g, pl.ds(0, seqs // 2 * unit), :]
        remote(whole, whole, xsend.at[0], xrecv.at[g], s, z).wait_recv()

    def turn_hidden(d):
        hidden_wait(d)
        hb[s, d] = hid[:, pl.ds(pl.multiple_of(d * rows + s * unit, 128), unit)]
        for i in range(seqs):
            ht[d * unit : (d + 1) * unit, i * tok : (i + 1) * tok] = hb[i, d].T

    slices = 4
    span_cols = gh.shape[1] // slices
    tall = min(512, span_cols)

    def spread(i):
        def step(j, carry):
            at = pl.multiple_of(i * span_cols + j * tall, tall)
            total = jnp.zeros((tok, tall), jnp.float32)
            for g in range(heads):
                grads = inside[:, g * duo : (g + 1) * duo]
                total = total + lax.dot_general(grads, w_ref[g, pl.ds(at, tall), :], nt, preferred_element_type=jnp.float32)
            gh[:, pl.ds(at, tall)] = total.astype(jnp.bfloat16)
            return carry

        lax.fori_loop(0, span_cols // tall, step, 0)

    def drain(ref, sem):
        remote(ref, ref, sem, wrecv.at[0, 0], s, z).wait_send()

    def drain_weights():
        wide = len([g for g in range(heads) if g in WIDE])
        for shard in range(groups):
            moved = w_ref.at[0, pl.ds(0, unit * (heads + wide)), :]

            @pl.when((shard <= z) & (z < last))
            def _():
                drain(moved, zsend.at[1, shard])

            @pl.when((shard >= z) & (z > 0))
            def _():
                drain(moved, zsend.at[0, shard])

        turns = groups - 1
        plane = heads * (seqs // 2 - 1) - wide
        drain(w_ref.at[pl.ds(0, turns), pl.ds(0, unit * plane), :], qsend.at[0])
        drain(w_ref.at[pl.ds(0, turns), pl.ds(0, unit * heads * (seqs // 2)), :], csend.at[0])

    def drain_tokens():
        drain(hb.at[pl.ds(0, seqs - 1)], hsend.at[0])
        for offset in range(1, reach + 1):

            @pl.when(linear + offset < devices)
            def _():
                drain(ret.at[offset - 1], ksend.at[offset - 1])

            @pl.when(linear >= offset)
            def _():
                drain(ret.at[offset - 1], bsend.at[offset - 1])

        drain(every.at[pl.ds(0, len(peers))], esend.at[0])
        drain(every.at[pl.ds(0, seqs // 2)], fsend.at[0])

    works = [own_send, forward, begin, cube_next, pair_send_after, pair_wait, project_chunk, attend_chunk, settle, widen, share]
    works += [product, hop, reduce, expand, relay, finish_chunk, spread, hidden_send, turn_hidden]
    fetched = False
    for place, *places in ORDER:
        if works[place] is attend_chunk and not fetched:
            loads[2].wait()
            loads[3].wait()
            fetched = True
        works[place](*places)
    drain_weights()
    drain_tokens()
    drain(wgb.at[:, pl.ds(0, len(peers) * unit), :], wsend.at[0])
    drain(wgb.at[:, pl.ds(0, seqs // 2 * unit), :], xsend.at[0])
    for d in range(groups):

        @pl.when(d > z)
        def _():
            drain(ups.at[:, d], usend.at[d])

        @pl.when(d < z)
        def _():
            drain(dns.at[:, d], dsend.at[d])


def fused(hidden, kv_blocks, kv_scale, queries, grad_out, reach):
    seqs = lax.axis_size("seq")
    groups = lax.axis_size("fsdp")
    tok, depth = hidden.shape
    rows, cols = kv_blocks.shape
    width = queries.shape[1]
    unit = rows // seqs
    heads = cols // (2 * HEAD)
    duo = 2 * HEAD
    count = (reach + 1) * tok
    bits = seqs.bit_length() - 1
    any_space = pl.BlockSpec(memory_space=pl.ANY)
    dma = pltpu.SemaphoreType.DMA
    b16 = lambda *shape: pltpu.VMEM(shape, jnp.bfloat16)
    f32 = lambda *shape: pltpu.VMEM(shape, jnp.float32)
    return pl.pallas_call(
        functools.partial(fused_kernel, seqs, groups, reach),
        out_shape=[b16(tok, width), b16(tok, width), b16(tok, depth), b16(heads, rows, duo)],
        in_specs=[any_space, any_space, pl.BlockSpec(memory_space=pltpu.SMEM), any_space, any_space],
        out_specs=[pl.BlockSpec(memory_space=pltpu.VMEM)] * 4,
        scratch_shapes=[
            b16(tok, depth), b16(rows, cols), b16(tok, width), b16(tok, width),
            b16(heads, depth, duo), b16(count, cols),
            b16(reach, tok, cols), b16(reach, tok, cols), f32(tok, cols), b16(seqs, tok, cols), b16(tok, cols),
            b16(seqs, groups, tok, unit), b16(groups * unit, seqs * tok), f32(heads, groups, unit, duo),
            b16(heads, groups, unit, duo), b16(heads, groups, unit, duo), b16(heads, groups, unit, duo), b16(heads, groups, unit, duo),
            f32(tok, tok), b16(unit, cols),
            dma((5,)), dma((2, groups)), dma((groups, heads)),
            dma((1,)), dma((groups - 1, heads, bits - 1)), dma((1,)), dma((groups - 1, heads)), dma((1,)), dma((groups,)),
            dma((reach,)), dma((heads, reach)), dma((reach,)), dma((heads, reach)),
            dma((1,)), dma((heads, 2)), dma((1,)), dma((heads,)),
            dma((groups,)), dma((heads, groups)), dma((groups,)), dma((heads, groups)),
            dma((1,)), dma((heads, 2)), dma((1,)), dma((heads,)),
        ],
        compiler_params=pltpu.CompilerParams(collective_id=0, has_side_effects=True, vmem_limit_bytes=VMEM_LIMIT),
        name="fused",
    )(hidden, kv_blocks, kv_scale.T, queries, grad_out)


def write_kernel(ao, dq, gh, wgb, ao_out, dq_out, gh_out, wg_out, wide, osem):
    parts, size, cols = wide.shape
    heads = wgb.shape[0]
    triples = ((ao, ao_out), (dq, dq_out), (gh, gh_out))
    stores = [pltpu.make_async_copy(src, dst, osem.at[parts + k]) for k, (src, dst) in enumerate(triples)]
    for copy in stores:
        copy.start()
    for p in range(parts):
        for g in range(heads):
            block = wgb[g, p * size : (p + 1) * size, :].astype(jnp.float32)
            wide[p, :, g * HEAD : (g + 1) * HEAD] = block[:, :HEAD]
            wide[p, :, (heads + g) * HEAD : (heads + g + 1) * HEAD] = block[:, HEAD:]
        store = pltpu.make_async_copy(wide.at[p], wg_out.at[pl.ds(p * size, size), :], osem.at[p])
        store.start()
        stores.append(store)
    for copy in stores:
        copy.wait()


def write(ao, dq, gh, wgb):
    parts = 8
    heads, rows, duo = wgb.shape
    any_space = pl.BlockSpec(memory_space=pl.ANY)
    return pl.pallas_call(
        write_kernel,
        out_shape=[jax.ShapeDtypeStruct(x.shape, x.dtype) for x in (ao, dq, gh)]
        + [jax.ShapeDtypeStruct((rows, heads * duo), jnp.float32)],
        in_specs=[pl.BlockSpec(memory_space=pltpu.VMEM)] * 4,
        out_specs=[any_space] * 4,
        scratch_shapes=[pltpu.VMEM((parts, rows // parts, heads * duo), jnp.float32), pltpu.SemaphoreType.DMA((parts + 3,))],
        compiler_params=pltpu.CompilerParams(vmem_limit_bytes=12 << 20),
        name="write",
    )(ao, dq, gh, wgb)


def body(hidden, kv_blocks, kv_scale, queries, grad_out):
    tok = hidden.shape[0]
    groups = lax.axis_size("fsdp")
    reach = groups // 2
    unit = kv_blocks.shape[0] // lax.axis_size("seq")
    heads = kv_blocks.shape[1] // (2 * HEAD)
    if unit % QB == 0 and (heads, groups, lax.axis_size("seq")) == PLANNED:
        outs = fused(hidden, kv_blocks, kv_scale, queries, grad_out, reach)
        return tuple(write(*outs))
    weights, kv, columns = project(hidden, kv_blocks, kv_scale)
    pieces = []
    for offset in range(reach, 0, -1):
        pieces.append(shifted(kv, ("seq", "fsdp"), offset))
    window = jnp.concatenate(pieces + [kv], axis=0)
    columns = columns.reshape(groups * tok, columns.shape[2])
    attn_out, grad_queries, dwin = attend(queries, window, grad_out, reach)
    back = dwin[: reach * tok].astype(jnp.bfloat16)
    own = dwin[reach * tok :]
    grad_hidden, weight_grad = finish(back, own, weights, columns, reach)
    return (attn_out, grad_queries, grad_hidden, weight_grad.astype(jnp.float32))


def solution(mesh):
    return jax.shard_map(
        body,
        mesh=mesh,
        in_specs=(
            P(("seq", "fsdp"), None),
            P("fsdp", None),
            P("fsdp", None),
            P(("seq", "fsdp"), None),
            P(("seq", "fsdp"), None),
        ),
        out_specs=(
            P(("seq", "fsdp"), None),
            P(("seq", "fsdp"), None),
            P(("seq", "fsdp"), None),
            P("fsdp", None),
        ),
        check_vma=False,
    )
```

profile of v0, /device:TPU:0, one launch (start us, length us, event | category | flops | bytes accessed | tf_op | source)
XLA Modules:
  0.0 146.6 jit_solution(13033404101276416333)
XLA Ops:
  0.6 141.3 %fused.1 = (bf16[128,4096]{1,0:T(8,128)(2,1)S(1)}, bf16[128,4096]{1,0:T(8,128)(2,1)S(1)}, bf16[128,8192]{1,0:T(8,128)(2,1)S(1)}, bf16[4,2048,256]{2,1,0:T(8,128)(2,1)S(1)}) custom-call(bf16[128,8192]{1,0:T(8,128)(2,1)} %hid_in.1, bf16[2048,1024]{1,0:T(8,128)(2,1)} %blk_in.1, f32[8,16]{1,0:T(8,128)} %bitcast.1, bf16[128,4096]{1,0:T(8,128)(2,1)} %q_in.1, ...), custom_call_target="tpu_custom_call" | custom-call | tf_op jit(solution)/shard_map/fused/pallas_call | solution.py:1085
  142.0 4.7 %write.1 = (bf16[128,4096]{1,0:T(8,128)(2,1)}, bf16[128,4096]{1,0:T(8,128)(2,1)}, bf16[128,8192]{1,0:T(8,128)(2,1)}, f32[2048,1024]{1,0:T(8,128)}) custom-call(bf16[128,4096]{1,0:T(8,128)(2,1)S(1)} %get-tuple-element.8.ao, bf16[128,4096]{1,0:T(8,128)(2,1)S(1)} %get-tuple-element.9.dq, bf16[128,8192]{1,0:T(8,128)(2,1)S(1)} %get-tuple-element.10.gh, ...), custom_call_target="tpu_custom_call" | custom-call | tf_op jit(solution)/shard_map/write/pallas_call | solution.py:1132
where the time goes:
time: 147 us
  Pallas kernels  146 us (99%)
    pallas_call x1, Pallas kernels, fused(): pl.pallas_call(functools.partial(fused_kernel, seqs, groups, reach), out_...  141 us
    pallas_call x1, Pallas kernels, write(): pl.pallas_call(write_kernel, out_shape=[jax.ShapeDtypeStruct(x.shape, x.d...  4.66 us

commit v1 on v0

--- a/solution.py
+++ b/solution.py
@@ -18,24 +18,24 @@
 (SEND, FORWARD, BEGIN, CUBE, PAIR, LAND, PROJECT, ATTEND, SETTLE, WIDEN, SHARE) = range(11)
 (PRODUCT, HOP, REDUCE, EXPAND, RELAY, FINISH, SPREAD, HIDDEN, TURN) = range(11, 20)
 VMEM_LIMIT = 50 << 20
+SPLIT = 2
 WIDE = (2,)
 ORDER = (
-    (HIDDEN, 3), (SEND, 1), (FORWARD, 1, 0), (FORWARD, 0, 0), (BEGIN, 1, 0), (SEND, 2), (FORWARD, 0, 1), (TURN, 3),
-    (BEGIN, 0, 0), (BEGIN, 0, 1), (SEND, 3), (CUBE, 1, 0), (CUBE, 0, 0), (FORWARD, 2, 0), (FORWARD, 0, 2),
-    (BEGIN, 2, 0), (FORWARD, 1, 1), (BEGIN, 0, 2), (CUBE, 0, 1), (FORWARD, 1, 2), (PAIR, 0, 2), (CUBE, 2, 0),
-    (BEGIN, 1, 2), (FORWARD, 2, 2), (BEGIN, 2, 2), (PAIR, 2, 0), (PAIR, 0, 0), (FORWARD, 1, 3), (BEGIN, 1, 3),
-    (PAIR, 0, 1), (BEGIN, 1, 1), (FORWARD, 0, 3), (PAIR, 1, 0), (LAND, 0, 1), (LAND, 0, 0), (LAND, 2, 0),
-    (FORWARD, 2, 1), (BEGIN, 0, 3), (BEGIN, 2, 1), (PAIR, 1, 2), (PAIR, 2, 2), (LAND, 1, 0), (FORWARD, 2, 3),
-    (PROJECT, 0), (BEGIN, 2, 3), (LAND, 0, 2), (LAND, 2, 2), (LAND, 1, 2), (CUBE, 1, 3), (CUBE, 0, 3), (PROJECT, 2),
-    (CUBE, 2, 3), (ATTEND, 0), (CUBE, 2, 1), (CUBE, 1, 1), (PAIR, 0, 3), (ATTEND, 2), (SETTLE, 0), (PAIR, 1, 3),
-    (PAIR, 2, 3), (TURN, 0), (HIDDEN, 2), (LAND, 1, 3), (LAND, 0, 3), (WIDEN, 0), (PAIR, 1, 1), (HIDDEN, 1),
-    (PAIR, 2, 1), (LAND, 2, 3), (PROJECT, 3), (LAND, 1, 1), (LAND, 2, 1), (PROJECT, 1), (ATTEND, 3), (TURN, 2),
-    (SHARE, 0), (ATTEND, 1), (SETTLE, 2), (TURN, 1), (PRODUCT, 0), (WIDEN, 2), (SHARE, 2), (PRODUCT, 2), (SETTLE, 1),
-    (SETTLE, 3), (HOP, 0, 1), (WIDEN, 1), (HOP, 0, 2), (SHARE, 1), (WIDEN, 3), (PRODUCT, 1), (HOP, 2, 1), (REDUCE, 0),
-    (SPREAD, 3), (EXPAND, 0), (SHARE, 3), (HOP, 2, 2), (SPREAD, 0), (HOP, 1, 1), (REDUCE, 2), (HOP, 1, 2),
-    (PRODUCT, 3), (EXPAND, 2), (RELAY, 0), (REDUCE, 1), (HOP, 3, 1), (RELAY, 2), (HOP, 3, 2), (EXPAND, 1),
-    (REDUCE, 3), (EXPAND, 3), (RELAY, 1), (SPREAD, 2), (SPREAD, 1), (FINISH, 2), (FINISH, 0), (RELAY, 3), (FINISH, 1),
-    (FINISH, 3),
+    (SEND, 3), (SEND, 1), (FORWARD, 0, 0), (BEGIN, 0, 0), (HIDDEN, 1), (FORWARD, 0, 3), (FORWARD, 1, 0),
+    (BEGIN, 0, 3), (BEGIN, 1, 0), (FORWARD, 1, 3), (CUBE, 0, 0), (FORWARD, 2, 0), (BEGIN, 2, 0), (FORWARD, 0, 1),
+    (CUBE, 1, 0), (BEGIN, 0, 1), (FORWARD, 1, 1), (SEND, 2), (BEGIN, 1, 1), (CUBE, 2, 0), (PAIR, 0, 0), (CUBE, 0, 3),
+    (BEGIN, 1, 3), (FORWARD, 2, 1), (PAIR, 1, 0), (BEGIN, 2, 1), (LAND, 1, 0), (LAND, 0, 0), (CUBE, 1, 1),
+    (FORWARD, 2, 3), (FORWARD, 0, 2), (BEGIN, 0, 2), (CUBE, 0, 1), (TURN, 0), (PAIR, 2, 0), (FORWARD, 1, 2),
+    (BEGIN, 2, 3), (LAND, 2, 0), (PROJECT, 0), (CUBE, 2, 1), (CUBE, 1, 3), (PAIR, 0, 3), (FORWARD, 2, 2), (ATTEND, 0),
+    (CUBE, 2, 3), (PAIR, 0, 2), (PAIR, 0, 1), (BEGIN, 1, 2), (TURN, 1), (PAIR, 2, 1), (PAIR, 1, 1), (LAND, 0, 1),
+    (LAND, 2, 1), (PAIR, 1, 3), (LAND, 1, 1), (LAND, 0, 3), (BEGIN, 2, 2), (PROJECT, 1), (SETTLE, 0), (LAND, 1, 3),
+    (PAIR, 2, 3), (LAND, 2, 3), (PAIR, 1, 2), (PROJECT, 3), (LAND, 1, 2), (LAND, 0, 2), (HIDDEN, 2), (PAIR, 2, 2),
+    (WIDEN, 0), (HIDDEN, 3), (LAND, 2, 2), (PROJECT, 2), (ATTEND, 1), (TURN, 2), (ATTEND, 3), (ATTEND, 2), (SHARE, 0),
+    (TURN, 3), (SETTLE, 1), (PRODUCT, 0), (WIDEN, 1), (HOP, 0, 1), (SHARE, 1), (SETTLE, 3), (HOP, 0, 2), (PRODUCT, 1),
+    (SETTLE, 2), (WIDEN, 3), (WIDEN, 2), (HOP, 1, 1), (SHARE, 3), (SPREAD, 0), (REDUCE, 0), (PRODUCT, 3), (SHARE, 2),
+    (HOP, 1, 2), (HOP, 3, 1), (REDUCE, 1), (EXPAND, 0), (HOP, 3, 2), (PRODUCT, 2), (REDUCE, 3), (EXPAND, 1),
+    (HOP, 2, 1), (HOP, 2, 2), (EXPAND, 3), (SPREAD, 3), (RELAY, 1), (REDUCE, 2), (SPREAD, 2), (RELAY, 3), (RELAY, 0),
+    (FINISH, 1), (EXPAND, 2), (FINISH, 3), (SPREAD, 1), (RELAY, 2), (FINISH, 0), (FINISH, 2),
 )
 
 
@@ -900,46 +900,56 @@
         for m in peers:
             every_pair(g, m, False).start()
 
-    def up_copy(g, d):
-        return remote(ups.at[g, d], upr.at[g, d], usend.at[d], urecv.at[g, d], s, z + 1)
-
-    def down_copy(g, d):
-        return remote(dns.at[g, d], dnr.at[g, d], dsend.at[d], drecv.at[g, d], s, z - 1)
+    part_rows = unit // SPLIT
+
+    def half_of(ref, g, d, q):
+        return ref.at[g, d, pl.ds(q * part_rows, part_rows), :]
+
+    def up_copy(g, d, q):
+        return remote(half_of(ups, g, d, q), half_of(upr, g, d, q), usend.at[d], urecv.at[g, d, q], s, z + 1)
+
+    def down_copy(g, d, q):
+        return remote(half_of(dns, g, d, q), half_of(dnr, g, d, q), dsend.at[d], drecv.at[g, d, q], s, z - 1)
+
+    def pass_on(g, d, up, adds):
+        source, here, copy = (ups, upr, up_copy) if up else (dns, dnr, down_copy)
+        for q in range(SPLIT):
+            cut = slice(q * part_rows, (q + 1) * part_rows)
+            value = part[g, d, cut]
+            if adds:
+                copy(g, d, q).wait_recv()
+                value = value + here[g, d, cut].astype(jnp.float32)
+            source[g, d, cut] = value.astype(jnp.bfloat16)
+            copy(g, d, q).start()
 
     def hop(g, k):
         @pl.when(z == k)
         def _():
             for d in range(last, k, -1):
-                value = part[g, d]
-                if k > 0:
-                    up_copy(g, d).wait_recv()
-                    value = value + upr[g, d].astype(jnp.float32)
-                ups[g, d] = value.astype(jnp.bfloat16)
-                up_copy(g, d).start()
+                pass_on(g, d, True, True)
 
         @pl.when(z == last - k)
         def _():
             for d in range(last - k):
-                value = part[g, d]
-                if k > 0:
-                    down_copy(g, d).wait_recv()
-                    value = value + dnr[g, d].astype(jnp.float32)
-                dns[g, d] = value.astype(jnp.bfloat16)
-                down_copy(g, d).start()
+                pass_on(g, d, False, True)
 
     def product(g):
         whole = every.at[pl.ds(0, seqs // 2), :, chunk(g)]
         remote(whole, whole, fsend.at[0], frecv.at[g], s, z).wait_recv()
         grads = every[:, :, g * duo : (g + 1) * duo].reshape(seqs * tok, duo)
-
-        def step(d, carry):
-            part[g, d] = jnp.dot(
-                ht[pl.ds(pl.multiple_of(d * unit, 128), unit), :], grads, preferred_element_type=jnp.float32
-            )
-            return carry
-
-        lax.fori_loop(0, groups, step, 0)
-        hop(g, 0)
+        for i in range(groups):
+            d = jnp.where(z == 0, last - i, i)
+            rows_of = pl.ds(pl.multiple_of(d * unit, 128), unit)
+            part[g, d] = jnp.dot(ht[rows_of, :], grads, preferred_element_type=jnp.float32)
+            if i < last:
+
+                @pl.when(z == 0)
+                def _():
+                    pass_on(g, last - i, True, False)
+
+                @pl.when(z == last)
+                def _():
+                    pass_on(g, i, False, False)
 
     def grad_copy(g, h, step, which):
         at = flipped(s, cube_mask(h, step, which)) * unit + h * (unit // 2)
@@ -959,11 +969,13 @@
     def reduce(g):
         @pl.when(z > 0)
         def _():
-            up_copy(g, z).wait_recv()
+            for q in range(SPLIT):
+                up_copy(g, z, q).wait_recv()
 
         @pl.when(z < last)
         def _():
-            down_copy(g, z).wait_recv()
+            for q in range(SPLIT):
+                down_copy(g, z, q).wait_recv()
 
         total = part[g, z] + upr[g, z].astype(jnp.float32) + dnr[g, z].astype(jnp.float32)
         wgb[g, pl.ds(pl.multiple_of(s * unit, 128), unit), :] = total.astype(jnp.bfloat16)
@@ -1098,7 +1110,7 @@
             dma((1,)), dma((groups - 1, heads, bits - 1)), dma((1,)), dma((groups - 1, heads)), dma((1,)), dma((groups,)),
             dma((reach,)), dma((heads, reach)), dma((reach,)), dma((heads, reach)),
             dma((1,)), dma((heads, 2)), dma((1,)), dma((heads,)),
-            dma((groups,)), dma((heads, groups)), dma((groups,)), dma((heads, groups)),
+            dma((groups,)), dma((heads, groups, SPLIT)), dma((groups,)), dma((heads, groups, SPLIT)),
             dma((1,)), dma((heads, 2)), dma((1,)), dma((heads,)),
         ],
         compiler_params=pltpu.CompilerParams(collective_id=0, has_side_effects=True, vmem_limit_bytes=VMEM_LIMIT),

time: 147 us -> 141 us (0.959)
  Pallas kernels: 146 us -> 140 us
    pallas_call x1, Pallas kernels: 141 us -> 135 us  [fused(): pl.pallas_call(functools.partial(fused_kernel, seqs, groups, reach), out_...]
where the time goes in v1:
time: 141 us; the launch traced here: 140 us
  Pallas kernels  140 us (99%)
    pallas_call x1, Pallas kernels, fused(): pl.pallas_call(functools.partial(fused_kernel, seqs, groups, reach), out_...  135 us
    pallas_call x1, Pallas kernels, write(): pl.pallas_call(write_kernel, out_shape=[jax.ShapeDtypeStruct(x.shape, x.d...  4.66 us

profile of v1, /device:TPU:0, one launch (start us, length us, event | category | flops | bytes accessed | tf_op | source)
XLA Modules:
  0.0 140.5 jit_solution(10176562845319567728)
XLA Ops:
  0.6 135.0 %fused.1 = (bf16[128,4096]{1,0:T(8,128)(2,1)S(1)}, bf16[128,4096]{1,0:T(8,128)(2,1)S(1)}, bf16[128,8192]{1,0:T(8,128)(2,1)S(1)}, bf16[4,2048,256]{2,1,0:T(8,128)(2,1)S(1)}) custom-call(bf16[128,8192]{1,0:T(8,128)(2,1)} %hid_in.1, bf16[2048,1024]{1,0:T(8,128)(2,1)} %blk_in.1, f32[8,16]{1,0:T(8,128)} %bitcast.1, bf16[128,4096]{1,0:T(8,128)(2,1)} %q_in.1, ...), custom_call_target="tpu_custom_call" | custom-call | tf_op jit(solution)/shard_map/fused/pallas_call | solution.py:1097
  135.7 4.7 %write.1 = (bf16[128,4096]{1,0:T(8,128)(2,1)}, bf16[128,4096]{1,0:T(8,128)(2,1)}, bf16[128,8192]{1,0:T(8,128)(2,1)}, f32[2048,1024]{1,0:T(8,128)}) custom-call(bf16[128,4096]{1,0:T(8,128)(2,1)S(1)} %get-tuple-element.8.ao, bf16[128,4096]{1,0:T(8,128)(2,1)S(1)} %get-tuple-element.9.dq, bf16[128,8192]{1,0:T(8,128)(2,1)S(1)} %get-tuple-element.10.gh, ...), custom_call_target="tpu_custom_call" | custom-call | tf_op jit(solution)/shard_map/write/pallas_call | solution.py:1144

commit v2 on v1

--- a/solution.py
+++ b/solution.py
@@ -21,21 +21,21 @@
 SPLIT = 2
 WIDE = (2,)
 ORDER = (
-    (SEND, 3), (SEND, 1), (FORWARD, 0, 0), (BEGIN, 0, 0), (HIDDEN, 1), (FORWARD, 0, 3), (FORWARD, 1, 0),
-    (BEGIN, 0, 3), (BEGIN, 1, 0), (FORWARD, 1, 3), (CUBE, 0, 0), (FORWARD, 2, 0), (BEGIN, 2, 0), (FORWARD, 0, 1),
-    (CUBE, 1, 0), (BEGIN, 0, 1), (FORWARD, 1, 1), (SEND, 2), (BEGIN, 1, 1), (CUBE, 2, 0), (PAIR, 0, 0), (CUBE, 0, 3),
-    (BEGIN, 1, 3), (FORWARD, 2, 1), (PAIR, 1, 0), (BEGIN, 2, 1), (LAND, 1, 0), (LAND, 0, 0), (CUBE, 1, 1),
-    (FORWARD, 2, 3), (FORWARD, 0, 2), (BEGIN, 0, 2), (CUBE, 0, 1), (TURN, 0), (PAIR, 2, 0), (FORWARD, 1, 2),
-    (BEGIN, 2, 3), (LAND, 2, 0), (PROJECT, 0), (CUBE, 2, 1), (CUBE, 1, 3), (PAIR, 0, 3), (FORWARD, 2, 2), (ATTEND, 0),
-    (CUBE, 2, 3), (PAIR, 0, 2), (PAIR, 0, 1), (BEGIN, 1, 2), (TURN, 1), (PAIR, 2, 1), (PAIR, 1, 1), (LAND, 0, 1),
-    (LAND, 2, 1), (PAIR, 1, 3), (LAND, 1, 1), (LAND, 0, 3), (BEGIN, 2, 2), (PROJECT, 1), (SETTLE, 0), (LAND, 1, 3),
-    (PAIR, 2, 3), (LAND, 2, 3), (PAIR, 1, 2), (PROJECT, 3), (LAND, 1, 2), (LAND, 0, 2), (HIDDEN, 2), (PAIR, 2, 2),
-    (WIDEN, 0), (HIDDEN, 3), (LAND, 2, 2), (PROJECT, 2), (ATTEND, 1), (TURN, 2), (ATTEND, 3), (ATTEND, 2), (SHARE, 0),
-    (TURN, 3), (SETTLE, 1), (PRODUCT, 0), (WIDEN, 1), (HOP, 0, 1), (SHARE, 1), (SETTLE, 3), (HOP, 0, 2), (PRODUCT, 1),
-    (SETTLE, 2), (WIDEN, 3), (WIDEN, 2), (HOP, 1, 1), (SHARE, 3), (SPREAD, 0), (REDUCE, 0), (PRODUCT, 3), (SHARE, 2),
-    (HOP, 1, 2), (HOP, 3, 1), (REDUCE, 1), (EXPAND, 0), (HOP, 3, 2), (PRODUCT, 2), (REDUCE, 3), (EXPAND, 1),
-    (HOP, 2, 1), (HOP, 2, 2), (EXPAND, 3), (SPREAD, 3), (RELAY, 1), (REDUCE, 2), (SPREAD, 2), (RELAY, 3), (RELAY, 0),
-    (FINISH, 1), (EXPAND, 2), (FINISH, 3), (SPREAD, 1), (RELAY, 2), (FINISH, 0), (FINISH, 2),
+    (SEND, 2), (FORWARD, 1, 0), (FORWARD, 0, 0), (BEGIN, 0, 0), (HIDDEN, 2), (FORWARD, 1, 2), (CUBE, 0, 0),
+    (BEGIN, 1, 0), (FORWARD, 0, 2), (FORWARD, 2, 0), (BEGIN, 0, 2), (FORWARD, 2, 2), (SEND, 1), (BEGIN, 1, 2),
+    (BEGIN, 2, 0), (SEND, 3), (CUBE, 1, 0), (FORWARD, 1, 3), (BEGIN, 2, 2), (FORWARD, 0, 3), (FORWARD, 0, 1),
+    (PAIR, 1, 2), (FORWARD, 1, 1), (PAIR, 1, 0), (CUBE, 2, 0), (BEGIN, 0, 3), (FORWARD, 2, 3), (PAIR, 2, 2),
+    (BEGIN, 0, 1), (PAIR, 0, 0), (TURN, 0), (LAND, 1, 0), (BEGIN, 1, 3), (PAIR, 0, 2), (LAND, 1, 2), (LAND, 0, 0),
+    (PAIR, 2, 0), (CUBE, 0, 3), (LAND, 2, 2), (LAND, 2, 0), (TURN, 2), (LAND, 0, 2), (FORWARD, 2, 1), (CUBE, 0, 1),
+    (PROJECT, 2), (PROJECT, 0), (BEGIN, 2, 3), (PAIR, 0, 3), (BEGIN, 2, 1), (CUBE, 1, 3), (BEGIN, 1, 1), (CUBE, 2, 3),
+    (ATTEND, 2), (PAIR, 1, 3), (CUBE, 1, 1), (ATTEND, 0), (PAIR, 0, 1), (CUBE, 2, 1), (PAIR, 2, 3), (SETTLE, 2),
+    (HIDDEN, 3), (LAND, 2, 3), (LAND, 1, 3), (LAND, 0, 3), (PROJECT, 3), (PAIR, 1, 1), (PAIR, 2, 1), (WIDEN, 2),
+    (LAND, 0, 1), (LAND, 1, 1), (LAND, 2, 1), (PROJECT, 1), (HIDDEN, 1), (ATTEND, 3), (SHARE, 2), (ATTEND, 1),
+    (TURN, 3), (SETTLE, 0), (TURN, 1), (PRODUCT, 2), (WIDEN, 0), (SETTLE, 3), (SETTLE, 1), (HOP, 2, 1), (WIDEN, 3),
+    (HOP, 2, 2), (SHARE, 0), (SPREAD, 2), (PRODUCT, 0), (REDUCE, 2), (SHARE, 3), (WIDEN, 1), (HOP, 0, 1), (EXPAND, 2),
+    (PRODUCT, 3), (SHARE, 1), (HOP, 0, 2), (REDUCE, 0), (HOP, 3, 1), (PRODUCT, 1), (HOP, 3, 2), (EXPAND, 0),
+    (RELAY, 2), (REDUCE, 3), (HOP, 1, 1), (HOP, 1, 2), (EXPAND, 3), (SPREAD, 0), (FINISH, 2), (REDUCE, 1),
+    (SPREAD, 3), (EXPAND, 1), (RELAY, 3), (RELAY, 0), (SPREAD, 1), (RELAY, 1), (FINISH, 3), (FINISH, 0), (FINISH, 1),
 )
 
 
@@ -682,19 +682,27 @@
             def _():
                 line_copy(z, 0, g, kind).start()
 
+    inner = (z > 0) & (z < last)
+
+    def line_wait(turn, g):
+        whole = w_ref.at[g, pl.ds(0, unit * (2 if g in WIDE else 1)), :]
+        remote(whole, whole, zsend.at[0, shards[turn]], zrecv.at[shards[turn], g], s, z).wait_recv()
+
     def forward(turn, g):
         shard = shards[turn]
-        whole = w_ref.at[g, pl.ds(0, unit * (2 if g in WIDE else 1)), :]
-        remote(whole, whole, zsend.at[0, shard], zrecv.at[shard, g], s, z).wait_recv()
-        for kind in kinds(g):
-
-            @pl.when((shard < z) & (z < last))
-            def _():
-                line_copy(shard, 1, g, kind).start()
-
-            @pl.when((shard > z) & (z > 0))
-            def _():
-                line_copy(shard, 0, g, kind).start()
+
+        @pl.when(inner)
+        def _():
+            line_wait(turn, g)
+            for kind in kinds(g):
+
+                @pl.when(shard < z)
+                def _():
+                    line_copy(shard, 1, g, kind).start()
+
+                @pl.when(shard > z)
+                def _():
+                    line_copy(shard, 0, g, kind).start()
 
     def cube_wait(turn, g, step):
         whole = w_ref.at[g, pl.ds(0, unit << step), :]
@@ -714,6 +722,10 @@
         remote(whole, whole, csend.at[0], crecv.at[turn, g], s, z).wait_recv()
 
     def begin(turn, g):
+        @pl.when(jnp.logical_not(inner))
+        def _():
+            line_wait(turn, g)
+
         if g not in WIDE:
             cube_send(turn, g, 0)
         else:

time: 141 us -> 140 us (level)
  no operation moved by 1% of the time
where the time goes in v2:
time: 140 us; the launch traced here: 139 us
  Pallas kernels  139 us (99%)
    pallas_call x1, Pallas kernels, fused(): pl.pallas_call(functools.partial(fused_kernel, seqs, groups, reach), out_...  134 us
    pallas_call x1, Pallas kernels, write(): pl.pallas_call(write_kernel, out_shape=[jax.ShapeDtypeStruct(x.shape, x.d...  4.66 us

profile of v2, /device:TPU:0, one launch (start us, length us, event | category | flops | bytes accessed | tf_op | source)
XLA Modules:
  0.0 139.3 jit_solution(17790961681959328820)
XLA Ops:
  0.6 133.9 %fused.1 = (bf16[128,4096]{1,0:T(8,128)(2,1)S(1)}, bf16[128,4096]{1,0:T(8,128)(2,1)S(1)}, bf16[128,8192]{1,0:T(8,128)(2,1)S(1)}, bf16[4,2048,256]{2,1,0:T(8,128)(2,1)S(1)}) custom-call(bf16[128,8192]{1,0:T(8,128)(2,1)} %hid_in.1, bf16[2048,1024]{1,0:T(8,128)(2,1)} %blk_in.1, f32[8,16]{1,0:T(8,128)} %bitcast.1, bf16[128,4096]{1,0:T(8,128)(2,1)} %q_in.1, ...), custom_call_target="tpu_custom_call" | custom-call | tf_op jit(solution)/shard_map/fused/pallas_call | solution.py:1109
  134.5 4.7 %write.1 = (bf16[128,4096]{1,0:T(8,128)(2,1)}, bf16[128,4096]{1,0:T(8,128)(2,1)}, bf16[128,8192]{1,0:T(8,128)(2,1)}, f32[2048,1024]{1,0:T(8,128)}) custom-call(bf16[128,4096]{1,0:T(8,128)(2,1)S(1)} %get-tuple-element.8.ao, bf16[128,4096]{1,0:T(8,128)(2,1)S(1)} %get-tuple-element.9.dq, bf16[128,8192]{1,0:T(8,128)(2,1)S(1)} %get-tuple-element.10.gh, ...), custom_call_target="tpu_custom_call" | custom-call | tf_op jit(solution)/shard_map/write/pallas_call | solution.py:1156

commit v3 on v2

--- a/solution.py
+++ b/solution.py
@@ -17,7 +17,7 @@
 PLANNED = (4, 4, 8)
 (SEND, FORWARD, BEGIN, CUBE, PAIR, LAND, PROJECT, ATTEND, SETTLE, WIDEN, SHARE) = range(11)
 (PRODUCT, HOP, REDUCE, EXPAND, RELAY, FINISH, SPREAD, HIDDEN, TURN) = range(11, 20)
-VMEM_LIMIT = 50 << 20
+VMEM_LIMIT = 51 << 20
 SPLIT = 2
 WIDE = (2,)
 ORDER = (
@@ -550,7 +550,7 @@
     seqs, groups, reach,
     hid_in, blk_in, sc_ref, q_in, g_in, ao, dq, gh, wgb,
     hid, blk, q_ref, g_ref, w_ref, win, back, ret, own, every, inside, hb, ht, part,
-    ups, upr, dns, dnr, bias, lead_ref,
+    ups, upr, dns, dnr, bias, lead_ref, sums,
     lsem, zsend, zrecv, qsend, qrecv, csend, crecv, hsend, hrecv, ksend, krecv, bsend, brecv,
     esend, erecv, fsend, frecv, usend, urecv, dsend, drecv, wsend, wrecv, xsend, xrecv,
 ):
@@ -720,6 +720,10 @@
     def pair_wait(turn, g):
         whole = w_ref.at[g, pl.ds(0, unit * (seqs // 2)), :]
         remote(whole, whole, csend.at[0], crecv.at[turn, g], s, z).wait_recv()
+        if g not in landed:
+            landed.add(g)
+            sums[g] = shard_product(g, z)
+        sums[g] += shard_product(g, shards[turn])
 
     def begin(turn, g):
         @pl.when(jnp.logical_not(inner))
@@ -782,14 +786,14 @@
         for g in range(heads):
             dnr[g, last] = jnp.zeros((unit, duo), jnp.bfloat16)
 
-    deep = min(1024, width)
+    landed = set()
+
+    def shard_product(g, shard):
+        at = pl.ds(pl.multiple_of(shard * rows, 128), rows)
+        return jnp.dot(hid[:, at], w_ref[g, at, :], preferred_element_type=jnp.float32)
 
     def project_chunk(g):
-        def step(i, total):
-            at = pl.multiple_of(i * deep, deep)
-            return total + jnp.dot(hid[:, pl.ds(at, deep)], w_ref[g, pl.ds(at, deep), :], preferred_element_type=jnp.float32)
-
-        total = lax.fori_loop(0, width // deep, step, jnp.zeros((tok, duo), jnp.float32))
+        total = sums[g]
         win[span:, g * duo : (g + 1) * duo] = total.astype(jnp.bfloat16)
         for offset in range(1, reach + 1):
 
@@ -1117,7 +1121,7 @@
             b16(reach, tok, cols), b16(reach, tok, cols), f32(tok, cols), b16(seqs, tok, cols), b16(tok, cols),
             b16(seqs, groups, tok, unit), b16(groups * unit, seqs * tok), f32(heads, groups, unit, duo),
             b16(heads, groups, unit, duo), b16(heads, groups, unit, duo), b16(heads, groups, unit, duo), b16(heads, groups, unit, duo),
-            f32(tok, tok), b16(unit, cols),
+            f32(tok, tok), b16(unit, cols), f32(heads, tok, duo),
             dma((5,)), dma((2, groups)), dma((groups, heads)),
             dma((1,)), dma((groups - 1, heads, bits - 1)), dma((1,)), dma((groups - 1, heads)), dma((1,)), dma((groups,)),
             dma((reach,)), dma((heads, reach)), dma((reach,)), dma((heads, reach)),

time: 140 us -> 142 us (1.014)
  Pallas kernels: 139 us -> 141 us
    pallas_call x1, Pallas kernels: 134 us -> 136 us  [fused(): pl.pallas_call(functools.partial(fused_kernel, seqs, groups, reach), out_...]
where the time goes in v3:
time: 142 us; the launch traced here: 141 us
  Pallas kernels  141 us (99%)
    pallas_call x1, Pallas kernels, fused(): pl.pallas_call(functools.partial(fused_kernel, seqs, groups, reach), out_...  136 us
    pallas_call x1, Pallas kernels, write(): pl.pallas_call(write_kernel, out_shape=[jax.ShapeDtypeStruct(x.shape, x.d...  4.66 us

profile of v3, /device:TPU:0, one launch (start us, length us, event | category | flops | bytes accessed | tf_op | source)
XLA Modules:
  0.0 141.4 jit_solution(6716598410886668004)
XLA Ops:
  0.6 135.9 %fused.1 = (bf16[128,4096]{1,0:T(8,128)(2,1)S(1)}, bf16[128,4096]{1,0:T(8,128)(2,1)S(1)}, bf16[128,8192]{1,0:T(8,128)(2,1)S(1)}, bf16[4,2048,256]{2,1,0:T(8,128)(2,1)S(1)}) custom-call(bf16[128,8192]{1,0:T(8,128)(2,1)} %hid_in.1, bf16[2048,1024]{1,0:T(8,128)(2,1)} %blk_in.1, f32[8,16]{1,0:T(8,128)} %bitcast.1, bf16[128,4096]{1,0:T(8,128)(2,1)} %q_in.1, ...), custom_call_target="tpu_custom_call" | custom-call | tf_op jit(solution)/shard_map/fused/pallas_call | solution.py:1113
  136.5 4.7 %write.1 = (bf16[128,4096]{1,0:T(8,128)(2,1)}, bf16[128,4096]{1,0:T(8,128)(2,1)}, bf16[128,8192]{1,0:T(8,128)(2,1)}, f32[2048,1024]{1,0:T(8,128)}) custom-call(bf16[128,4096]{1,0:T(8,128)(2,1)S(1)} %get-tuple-element.8.ao, bf16[128,4096]{1,0:T(8,128)(2,1)S(1)} %get-tuple-element.9.dq, bf16[128,8192]{1,0:T(8,128)(2,1)S(1)} %get-tuple-element.10.gh, ...), custom_call_target="tpu_custom_call" | custom-call | tf_op jit(solution)/shard_map/write/pallas_call | solution.py:1160
